TPU v7x, 32 devices: a whole 2x2x4 slice. The times are simulated.
32 devices in a mesh: seq: 4 (over y, core), blk: 8 (over z, x).
Axes of the slice: x: 2, y: 2, z: 4, core: 2. Of those that a mesh axis runs over, the one named last changes fastest.
Arguments:
- kv_cache: bfloat16 [4, 2, 16, 4096, 1024], P(None, None, None, ('seq', 'blk')), may hold values from -18 to 18, as said below
- queries: bfloat16 [4, 128, 1024], P(None, 'blk'), may hold values from -400 to 400
- fresh_key_value: bfloat16 [4, 2, 128, 128], P(None, None, 'blk'), may hold values from -70 to 70
- lengths: int32 [16], replicated, may hold values from 1 to 4096, 49152 in all
Outputs:
- quant_cache: bfloat16 [4, 2, 128, 4096, 128], P(None, None, 'blk', 'seq')
- block_scale: float32 [4, 2, 128, 32], P(None, None, 'blk', 'seq')
- attended: bfloat16 [4, 128, 1024], P(None, 'blk')
Inputs may be any that keep to these rules, and one draw needn't show every extreme that they name: `kv_cache`: each entry is a random value times a factor drawn for its position and head. `lengths`: every sequence has at least one live position, and some sequence uses all 4096.
All inputs are finite; a program needn't handle non-finite values.
Results may differ from a plain program's by a relative error of at most 0.003.
The roundings to bfloat16 on the way count: a program that leaves them out, or rounds other values in their place, can miss the bound.
Values may be sent and summed in bfloat16 or wider, within the bound.
A program may use at most 192 MiB of HBM per device.

v0:
```python
import jax
import jax.numpy as jnp
from jax import lax
from jax.sharding import PartitionSpec as P

HEAD_DIM = 128
QUERY_GROUP = 8
BLOCK = 128


def on_device(kv_cache, queries, fresh_key_value, lengths):
    layers, _, batch, local_rows, width = kv_cache.shape
    heads = width // HEAD_DIM
    blk_count = lax.axis_size("blk")
    blk_place = lax.axis_index("blk")
    pairs_here = heads * batch // blk_count
    seq_rows = local_rows * blk_count
    blocks_here = seq_rows // BLOCK
    arranged = kv_cache.reshape(layers, 2, batch, local_rows, heads, HEAD_DIM).transpose(
        0, 1, 4, 2, 3, 5
    )
    arranged = arranged.reshape(layers, 2, heads * batch, local_rows, HEAD_DIM)
    pair_start = blk_place * pairs_here
    moved = lax.all_to_all(arranged, "blk", split_axis=2, concat_axis=3, tiled=True)
    grouped = moved.reshape(layers, 2, pairs_here, blocks_here, BLOCK, HEAD_DIM)
    block_scale = (
        jnp.maximum(jnp.max(jnp.abs(grouped), axis=(4, 5)).astype(jnp.float32), 1.0) / 127.0
    )
    quant = (grouped.astype(jnp.float32) / block_scale[..., None, None]).astype(jnp.bfloat16)
    quant = quant.reshape(layers, 2, pairs_here, seq_rows, HEAD_DIM)
    seq_start = lax.axis_index("seq") * seq_rows
    pair_len = lax.dynamic_slice_in_dim(jnp.tile(lengths, heads), pair_start, pairs_here)
    positions = seq_start + jnp.arange(seq_rows, dtype=jnp.int32).reshape(blocks_here, BLOCK)
    valid = positions[None] < pair_len[:, None, None]
    inverse = 1.0 / jnp.sqrt(jnp.float32(HEAD_DIM))
    grouped_queries = queries.reshape(layers, pairs_here, QUERY_GROUP, HEAD_DIM)
    peaks = []
    totals = []
    sums = []
    for layer in range(layers):
        raw = jnp.einsum(
            "pgd,prd->pgr",
            grouped_queries[layer],
            quant[layer, 0],
            preferred_element_type=jnp.float32,
        )
        scores = (
            raw.reshape(pairs_here, QUERY_GROUP, blocks_here, BLOCK)
            * block_scale[layer, 0][:, None, :, None]
            * inverse
        )
        masked = jnp.where(valid[:, None], scores, -1e30)
        block_top = jnp.max(masked, axis=-1)
        weight = jnp.where(valid[:, None], jnp.exp(masked - block_top[..., None]), 0.0)
        block_total = jnp.sum(weight, axis=-1)
        rounded = (weight * block_scale[layer, 1][:, None, :, None]).astype(jnp.bfloat16)
        values = quant[layer, 1].reshape(pairs_here, blocks_here, BLOCK, HEAD_DIM)
        block_sum = jnp.einsum(
            "pgnt,pntd->pgnd", rounded, values, preferred_element_type=jnp.float32
        )
        local_top = jnp.max(block_top, axis=-1)
        scale_factor = jnp.exp(block_top - local_top[..., None])
        peaks.append(local_top)
        totals.append(jnp.sum(scale_factor * block_total, axis=-1))
        sums.append(jnp.sum(scale_factor[..., None] * block_sum, axis=2))
    peak = jnp.stack(peaks)
    total = jnp.stack(totals)
    weighted = jnp.stack(sums)
    shared_top = lax.pmax(peak, "seq")
    scale_factor = jnp.exp(peak - shared_top)
    total, weighted = lax.psum((total * scale_factor, weighted * scale_factor[..., None]), "seq")
    peak = shared_top
    own = (
        jnp.einsum(
            "lpgd,lpd->lpg",
            grouped_queries,
            fresh_key_value[:, 0],
            preferred_element_type=jnp.float32,
        )
        * inverse
    )
    top = jnp.maximum(peak, own)
    cache_w = jnp.exp(peak - top)
    own_w = jnp.exp(own - top)
    numer = (
        weighted * cache_w[..., None]
        + own_w[..., None] * fresh_key_value[:, 1].astype(jnp.float32)[:, :, None, :]
    )
    denom = total * cache_w + own_w
    attended = (
        (numer / denom[..., None])
        .reshape(layers, pairs_here, QUERY_GROUP * HEAD_DIM)
        .astype(jnp.bfloat16)
    )
    return (quant, block_scale, attended)


def solution(mesh):
    in_specs = (
        P(None, None, None, ("seq", "blk"), None),
        P(None, "blk", None),
        P(None, None, "blk", None),
        P(),
    )
    out_specs = (
        P(None, None, "blk", "seq", None),
        P(None, None, "blk", "seq"),
        P(None, "blk", None),
    )
    return jax.shard_map(
        on_device, mesh=mesh, in_specs=in_specs, out_specs=out_specs, check_vma=False
    )
```

profile of v0, /device:TPU:1, one launch (start us, length us, event | category | flops | bytes accessed | tf_op | source)
XLA Modules:
  0.0 1026.3 jit_solution(197977357570739834)
XLA Ops:
  7.2 43.9 %copy.101 = bf16[4,2,16,128,1024]{3,4,2,1,0:T(8,128)(2,1)} copy(bf16[4,2,16,128,1024]{4,3,2,1,0:T(8,128)(2,1)} %param.4) | data formatting | bytes 67108864 | tf_op args[0]
  51.0 42.3 %copy.102 = bf16[4,2,8,16,128,128]{5,4,3,2,1,0:T(8,128)(2,1)} copy(bf16[4,2,8,16,128,128]{4,5,2,3,1,0:T(8,128)(2,1)} %bitcast.243) | data formatting | bytes 67108864 | tf_op jit(solution)/shard_map/transpose | solution.py:19
  93.4 22.9 %copy.103 = bf16[4,2,128,128,128]{4,3,1,0,2:T(8,128)(2,1)} copy(bf16[4,2,128,128,128]{4,3,2,1,0:T(8,128)(2,1)} %bitcast.241) | data formatting | bytes 67108864 | tf_op jit(solution)/shard_map/reshape | solution.py:22
  116.3 7.2 all-to-all-start
  124.4 722.3 %all-to-all-done = bf16[4,2,128,128,128]{4,3,1,0,2:T(8,128)(2,1)} async-done(((bf16[4,2,128,128,128]{4,3,1,0,2:T(8,128)(2,1)}), bf16[4,2,128,128,128]{4,3,1,0,2:T(8,128)(2,1)}, u32[]{:S(2)}, u32[]{:S(2)}) %all-to-all-start) | async-done | bytes 33554464 | tf_op jit(solution)/shard_map/all_to_all | solution.py:24
  846.6 11.5 %abs_reduce_fusion = bf16[4,2,128]{1,0,2:T(4,128)(2,1)S(1)} fusion(bf16[4,2,128,128,128]{4,3,1,0,2:T(8,128)(2,1)} %all-to-all-done), kind=kLoop, calls=%fused_computation.3 | loop fusion | flops 33553408 | bytes 33556480 | tf_op jit(solution)/shard_map/reduce_max | solution.py:27
  858.5 23.0 %copy.104 = bf16[4,2,128,128,128]{4,3,2,1,0:T(8,128)(2,1)} copy(bf16[4,2,128,128,128]{4,3,1,0,2:T(8,128)(2,1)} %all-to-all-done) | data formatting | bytes 67108864 | tf_op jit(solution)/shard_map/all_to_all | solution.py:24
  881.6 23.3 %fusion.1 = bf16[4,2,16,8,128,128]{5,4,2,3,1,0:T(8,128)(2,1)} fusion(bf16[4,2,8,16,128,128]{5,4,3,2,1,0:T(8,128)(2,1)} %bitcast.242, f32[4,2,16,8]{2,3,1,0:T(8,128)S(1)} %bitcast.258), kind=kLoop, calls=%fused_computation.2 | loop fusion | flops 50331648 | bytes 67112960 | tf_op jit(solution)/shard_map/convert_element_type | solution.py:29
  904.9 22.9 %copy.106 = bf16[4,2,16,8,128,128]{5,4,3,2,1,0:T(8,128)(2,1)} copy(bf16[4,2,16,8,128,128]{5,4,2,3,1,0:T(8,128)(2,1)} %fusion.1) | data formatting | bytes 67108864 | tf_op jit(solution)/shard_map/convert_element_type | solution.py:29
  927.8 12.2 %fusion.90 = (bf16[1,1,16,1024,128]{4,3,2,1,0:T(8,128)(2,1)}, bf16[1,1,16,1024,128]{4,3,2,1,0:T(8,128)(2,1)}, bf16[1,1,16,1024,128]{4,3,2,1,0:T(8,128)(2,1)}, bf16[1,1,16,1024,128]{4,3,2,1,0:T(8,128)(2,1)}) fusion(bf16[4,2,16,1024,128]{4,3,2,1,0:T(8,128)(2,1)} %bitcast.244), kind=kLoop, calls=%fused_computation.153 | loop fusion | bytes 33554432 | tf_op jit(solution)/shard_map/slice | solution.py:57
  939.9 3.4 fusion.2
  943.3 3.4 fusion.3
  947.3 3.5 fusion.38
  950.8 3.1 fusion.34
  954.8 10.3 %pmax.7 = f32[4,16,8]{1,2,0:T(8,128)S(1)} all-reduce(f32[4,16,8]{1,2,0:T(8,128)S(1)} %pad_maximum_fusion), channel_id=1, replica_groups=mesh['seq'=4,'blk'=8] {'seq'}, use_global_device_ids=true, to_apply=%region_13.14 | all-reduce | flops 512 | bytes 4096 | tf_op jit(solution)/shard_map/pmax | solution.py:69
  965.1 1.5 fusion.35
  967.0 10.3 %psum.15 = f32[4,16,8]{1,2,0:T(8,128)S(1)} all-reduce(f32[4,16,8]{1,2,0:T(8,128)S(1)} %get-tuple-element.17), channel_id=1, replica_groups=mesh['seq'=4,'blk'=8] {'seq'}, use_global_device_ids=true, to_apply=%region_23.24 | all-reduce | flops 512 | bytes 4096 | tf_op jit(solution)/shard_map/psum | solution.py:71
  977.7 3.6 fusion.13
  981.3 1.3 fusion.12
  982.6 0.9 copy-done.1
  983.5 1.3 fusion.11
  985.0 1.3 fusion.10
  987.4 30.1 %all-reduce.2.cloned.1.call-done = f32[4,16,8,128]{3,2,1,0:T(8,128)} async-done(((f32[4,16,8,128]{3,2,1,0:T(8,128)}), f32[4,16,8,128]{3,2,1,0:T(8,128)}) %all-reduce.2.cloned.1.call-update) | async-done | bytes 262160 | tf_op jit(solution)/shard_map/psum | solution.py:71
  1017.5 1.2 divide_convert_fusion
  (70 shorter events, 5.5 us)
Async XLA Ops:
  116.3 7.3 copy-start.6
  116.3 7.4 copy-start.3
  116.3 7.5 copy-start.5
  116.3 730.3 %all-to-all-start = ((bf16[4,2,128,128,128]{4,3,1,0,2:T(8,128)(2,1)}), bf16[4,2,128,128,128]{4,3,1,0,2:T(8,128)(2,1)}, u32[]{:S(2)}, u32[]{:S(2)}) async-start(bf16[4,2,128,128,128]{4,3,1,0,2:T(8,128)(2,1)} %copy.103), calls=%async_computation | async-start | bytes 67108864 | tf_op jit(solution)/shard_map/all_to_all | solution.py:24
  123.5 894.0 %all-reduce.2.cloned.1.call-start = ((), (), s32[]{:S(2)}) async-start(), calls=%async_computation.1 | async-start | bytes 524288 | tf_op jit(solution)/shard_map/psum | solution.py:71
  858.4 23.1 %copy-start.4 = (f32[4,2,8,16]{3,2,1,0:T(8,128)}, f32[4,2,8,16]{3,2,1,0:T(8,128)S(1)}, u32[]{:S(2)}) copy-start(f32[4,2,8,16]{3,2,1,0:T(8,128)S(1)} %copy.105) | copy-start | bytes 12292
  977.7 3.6 copy-start.2
  981.3 2.2 copy-start.1
  982.6 2.4 copy-start
Sparse Core Ops, SparseCore 0:
  987.3 30.1 all-reduce.1
where the time goes:
time: 1030 us
  waiting for transfers between devices  752 us (73%)
  local copies, waits for them, and re-layouts  171 us (17%)
  other arithmetic  39.3 us (4%)
  matrix products  21.1 us (2%)
  blocking collectives  20.6 us (2%)
  between operations  14.3 us (1%)
    all_to_all x1, waiting for transfers between devices, on_device(): lax.all_to_all(arranged, 'blk', split_axis=2, concat_axis=3, tiled=True)  722 us
    unnamed x25, local copies, waits for them, and re-layouts  45.2 us
    transpose x1, local copies, waits for them, and re-layouts, on_device(): kv_cache.reshape(layers, 2, batch, local_rows, heads, HEAD_DIM)  42.3 us
    psum x1, waiting for transfers between devices, on_device(): lax.psum((total * scale_factor, weighted * scale_factor[..., None]), 'seq')  30.1 us
    convert_element_type x1, other arithmetic, on_device(): (grouped.astype(jnp.float32) / block_scale[..., None, None]).astype(jnp.b...  23.3 us
    all_to_all x1, local copies, waits for them, and re-layouts, on_device(): lax.all_to_all(arranged, 'blk', split_axis=2, concat_axis=3, tiled=True)  23 us
    reshape x1, local copies, waits for them, and re-layouts, on_device(): arranged = arranged.reshape(layers, 2, heads * batch, local_rows, HEAD_DIM)  22.9 us
    convert_element_type x1, local copies, waits for them, and re-layouts, on_device(): (grouped.astype(jnp.float32) / block_scale[..., None, None]).astype(jnp.b...  22.9 us
  transfers between devices with their start and end apart: 2, of which 2 were waited for; matrix products, arithmetic and copies ran while one was open for 0% of the time, Pallas kernels for 0%

commit v1 on v0

v1 whole, which is shorter than its diff:
```python
import functools

import jax
import jax.numpy as jnp
from jax import lax
from jax.experimental import pallas as pl
from jax.experimental.pallas import tpu as pltpu
from jax.sharding import PartitionSpec as P

HEAD_DIM = 128
QUERY_GROUP = 8
BLOCK = 128
MESH = pl.DeviceIdType.MESH


def gather_kernel(x_ref, o_ref):
    o_ref[0] = x_ref[0]


def gather_parts(kv_cache, layer, s0, ns, owners):
    layers, _, batch, rows, width = kv_cache.shape
    pairs = (width // HEAD_DIM) * batch // owners

    def in_map(j):
        first = j * pairs + s0
        return (layer, 0, (first % batch) // ns, 0, first // batch)

    shape = (owners, 2, ns, rows, HEAD_DIM)
    size = owners * 2 * ns * rows * HEAD_DIM * 2
    return pl.pallas_call(
        gather_kernel,
        grid=(owners,),
        in_specs=[pl.BlockSpec((1, 2, ns, rows, HEAD_DIM), in_map)],
        out_specs=pl.BlockSpec((1, 2, ns, rows, HEAD_DIM), lambda j: (j, 0, 0, 0, 0)),
        out_shape=jax.ShapeDtypeStruct(shape, kv_cache.dtype),
        cost_estimate=pl.CostEstimate(flops=0, bytes_accessed=2 * size, transcendentals=0),
        compiler_params=pltpu.CompilerParams(vmem_limit_bytes=16 << 20),
    )(kv_cache)


def attend_kernel(s0, step_pairs, left_ref, x_ref, q_ref, *rest):
    quant_ref, scale_ref, stat_ref = rest[-3:]
    parts, _, _, rows, _ = x_ref.shape
    blocks = parts * rows // BLOCK
    inverse = 1.0 / (float(HEAD_DIM) ** 0.5)
    per_block = max(1, BLOCK // rows)
    lane = lax.broadcasted_iota(jnp.int32, (QUERY_GROUP, BLOCK), 1)
    lane_row = lax.broadcasted_iota(jnp.int32, (1, blocks), 1)

    def take(c, s, n):
        if rows >= BLOCK:
            inside = rows // BLOCK
            lo = (n % inside) * BLOCK
            return x_ref[n // inside, c, s, lo : lo + BLOCK, :]
        piece = x_ref[n * per_block : (n + 1) * per_block, c, s, :, :]
        return piece.reshape(BLOCK, HEAD_DIM)

    for s in range(step_pairs):
        live = left_ref[s0 + pl.program_id(0) * step_pairs + s]
        scales = [[], []]
        for c in range(2):
            row = jnp.zeros((1, blocks), jnp.float32)
            for n in range(blocks):
                piece = take(c, s, n)
                top = jnp.max(jnp.abs(piece), axis=0, keepdims=True)
                top = jnp.max(top.astype(jnp.float32), axis=1, keepdims=True)
                scale = jnp.maximum(top, 1.0) / 127.0
                quant = piece.astype(jnp.float32) * (1.0 / scale)
                quant_ref[0, c, s, n * BLOCK : (n + 1) * BLOCK, :] = quant.astype(jnp.bfloat16)
                scales[c].append(scale)
                row = jnp.where(lane_row == n, scale, row)
            scale_ref[s, c : c + 1, :] = row
        raw = lax.dot_general(
            q_ref[0, s],
            quant_ref[0, 0, s],
            (((1,), (1,)), ((), ())),
            preferred_element_type=jnp.float32,
        )
        peaks, totals, sums = [], [], []
        for n in range(blocks):
            score = raw[:, n * BLOCK : (n + 1) * BLOCK] * (scales[0][n] * inverse)
            valid = lane + n * BLOCK < live
            score = jnp.where(valid, score, -1e30)
            peak = jnp.max(score, axis=1, keepdims=True)
            weight = jnp.where(valid, jnp.exp(score - peak), 0.0)
            peaks.append(peak)
            totals.append(jnp.sum(weight, axis=1, keepdims=True))
            rounded = (weight * scales[1][n]).astype(jnp.bfloat16)
            sums.append(
                jnp.dot(
                    rounded,
                    quant_ref[0, 1, s, n * BLOCK : (n + 1) * BLOCK, :],
                    preferred_element_type=jnp.float32,
                )
            )
        top = functools.reduce(jnp.maximum, peaks)
        total = jnp.zeros_like(top)
        numer = jnp.zeros((QUERY_GROUP, HEAD_DIM), jnp.float32)
        for n in range(blocks):
            factor = jnp.exp(peaks[n] - top)
            total = total + factor * totals[n]
            numer = numer + factor * sums[n]
        stat_ref[s, 0] = numer
        stat_ref[s, 1] = jnp.where(lane < BLOCK // 2, top, total)


def attend(left, moved, queries, quant, out_shape, layer, s0):
    owners, _, ns, rows, _ = moved.shape
    seq_rows = owners * rows
    blocks = seq_rows // BLOCK
    step_pairs = 2 if ns % 2 == 0 else 1
    size = 2 * ns * seq_rows * HEAD_DIM * 2
    first = s0 // step_pairs
    in_specs = [
        pl.BlockSpec((owners, 2, step_pairs, rows, HEAD_DIM), lambda i, left: (0, 0, i, 0, 0)),
        pl.BlockSpec(
            (1, step_pairs, QUERY_GROUP, HEAD_DIM), lambda i, left: (layer, first + i, 0, 0)
        ),
    ]
    operands = [left, moved, queries]
    aliases = {}
    if quant is not None:
        in_specs.append(pl.BlockSpec(memory_space=pl.ANY))
        operands.append(quant)
        aliases = {3: 0}
    return pl.pallas_call(
        functools.partial(attend_kernel, s0, step_pairs),
        grid_spec=pltpu.PrefetchScalarGridSpec(
            num_scalar_prefetch=1,
            grid=(ns // step_pairs,),
            in_specs=in_specs,
            out_specs=[
                pl.BlockSpec(
                    (1, 2, step_pairs, seq_rows, HEAD_DIM),
                    lambda i, left: (layer, 0, first + i, 0, 0),
                ),
                pl.BlockSpec((step_pairs, 2, blocks), lambda i, left: (i, 0, 0)),
                pl.BlockSpec(
                    (step_pairs, 2, QUERY_GROUP, HEAD_DIM), lambda i, left: (i, 0, 0, 0)
                ),
            ],
        ),
        out_shape=[
            jax.ShapeDtypeStruct(out_shape, jnp.bfloat16),
            jax.ShapeDtypeStruct((ns, 2, blocks), jnp.float32),
            jax.ShapeDtypeStruct((ns, 2, QUERY_GROUP, HEAD_DIM), jnp.float32),
        ],
        input_output_aliases=aliases,
        cost_estimate=pl.CostEstimate(
            flops=4 * size * QUERY_GROUP, bytes_accessed=2 * size, transcendentals=0
        ),
        compiler_params=pltpu.CompilerParams(vmem_limit_bytes=24 << 20),
    )(*operands)


def combine_kernel(stat_ref, q_ref, fresh_ref, o_ref, held, send_sem, recv_sem):
    ranges = lax.axis_size("seq")
    me = lax.axis_index("seq")
    amount = stat_ref.shape[0]
    inverse = 1.0 / (float(HEAD_DIM) ** 0.5)
    barrier = pltpu.get_barrier_semaphore()
    for k in range(1, ranges):
        pl.semaphore_signal(
            barrier, inc=1, device_id={"seq": (me + k) % ranges}, device_id_type=MESH
        )
    pl.semaphore_wait(barrier, ranges - 1)
    copies = []
    for k in range(1, ranges):
        copy = pltpu.make_async_remote_copy(
            src_ref=stat_ref,
            dst_ref=held.at[me],
            send_sem=send_sem.at[k - 1],
            recv_sem=recv_sem.at[k - 1],
            device_id={"seq": (me + k) % ranges},
            device_id_type=MESH,
        )
        copy.start()
        copies.append(copy)
    held[me] = stat_ref[...]
    for copy in copies:
        copy.wait()

    def one(i, carry):
        query = q_ref[i].astype(jnp.float32)
        fresh_key = fresh_ref[i, 0:1, :]
        fresh_value = fresh_ref[i, 1:2, :]
        own = jnp.sum(query * fresh_key, axis=1, keepdims=True) * inverse
        tails = [held[r, i, 1] for r in range(ranges)]
        tops = [tail[:, 0:1] for tail in tails]
        top = functools.reduce(jnp.maximum, tops, own)
        own_weight = jnp.exp(own - top)
        numer = own_weight * fresh_value
        denom = own_weight
        for r in range(ranges):
            factor = jnp.exp(tops[r] - top)
            numer = numer + factor * held[r, i, 0]
            denom = denom + factor * tails[r][:, BLOCK // 2 : BLOCK // 2 + 1]
        o_ref[i] = (numer / denom).astype(jnp.bfloat16)
        return carry

    lax.fori_loop(0, amount, one, 0)


def combine(stat, queries, fresh, ident):
    amount = stat.shape[0]
    ranges = lax.axis_size("seq")
    return pl.pallas_call(
        combine_kernel,
        in_specs=[pl.BlockSpec(memory_space=pltpu.VMEM)] * 3,
        out_specs=pl.BlockSpec(memory_space=pltpu.VMEM),
        out_shape=jax.ShapeDtypeStruct((amount, QUERY_GROUP, HEAD_DIM), jnp.bfloat16),
        scratch_shapes=[
            pltpu.VMEM((ranges, *stat.shape), jnp.float32),
            pltpu.SemaphoreType.DMA((ranges - 1,)),
            pltpu.SemaphoreType.DMA((ranges - 1,)),
        ],
        cost_estimate=pl.CostEstimate(
            flops=0, bytes_accessed=stat.size * 4 * ranges, transcendentals=0
        ),
        compiler_params=pltpu.CompilerParams(
            collective_id=ident, has_side_effects=True, vmem_limit_bytes=16 << 20
        ),
    )(stat, queries, fresh)


def on_device(kv_cache, queries, fresh_key_value, lengths):
    layers, _, batch, rows, width = kv_cache.shape
    heads = width // HEAD_DIM
    owners = lax.axis_size("blk")
    pairs = heads * batch // owners
    seq_rows = rows * owners
    blocks = seq_rows // BLOCK
    first_pair = lax.axis_index("blk") * pairs
    left = lengths[(first_pair + jnp.arange(pairs, dtype=jnp.int32)) % batch]
    left = left - lax.axis_index("seq") * seq_rows
    grouped = queries.reshape(layers, pairs, QUERY_GROUP, HEAD_DIM)
    chunks = [(layer, 0, pairs) for layer in range(layers)]
    out_shape = (layers, 2, pairs, seq_rows, HEAD_DIM)

    quant = None
    scales, stats = [], []
    for layer, s0, ns in chunks:
        sent = gather_parts(kv_cache, layer, s0, ns, owners)
        moved = lax.all_to_all(sent, "blk", split_axis=0, concat_axis=0, tiled=True)
        quant, scale, stat = attend(left, moved, grouped, quant, out_shape, layer, s0)
        scales.append(scale)
        stats.append(stat)
    fresh = fresh_key_value.transpose(0, 2, 1, 3).astype(jnp.float32)
    early = layers - 1
    outs = []
    for ident, (lo, hi) in enumerate([(0, early), (early, layers)]):
        amount = (hi - lo) * pairs
        outs.append(
            combine(
                jnp.concatenate(stats[lo:hi], axis=0),
                grouped[lo:hi].reshape(amount, QUERY_GROUP, HEAD_DIM),
                fresh[lo:hi].reshape(amount, 2, HEAD_DIM),
                ident,
            ).reshape(hi - lo, pairs, QUERY_GROUP * HEAD_DIM)
        )
    attended = jnp.concatenate(outs, axis=0)
    block_scale = jnp.stack(scales).transpose(0, 2, 1, 3)
    return quant, block_scale, attended


def solution(mesh):
    in_specs = (
        P(None, None, None, ("seq", "blk"), None),
        P(None, "blk", None),
        P(None, None, "blk", None),
        P(),
    )
    out_specs = (
        P(None, None, "blk", "seq", None),
        P(None, None, "blk", "seq"),
        P(None, "blk", None),
    )
    return jax.shard_map(
        on_device, mesh=mesh, in_specs=in_specs, out_specs=out_specs, check_vma=False
    )
```

time: 1030 us -> 788 us (0.77)
  local copies, waits for them, and re-layouts: 171 us -> 14.8 us
  waiting for transfers between devices: 752 us -> 631 us
  Pallas kernels: 0 us -> 116 us
  other arithmetic: 39.3 us -> 0.75 us
  matrix products: 21.1 us -> 0 us
  blocking collectives: 20.6 us -> 0 us
  starting transfers between devices: 7.25 us -> 22.7 us
  between operations: 14.3 us -> 0.87 us
    pallas_call x0 -> x10, Pallas kernels: none -> 116 us  [the longest x4 48.5 us: attend(): pl.pallas_call(functools.partial(attend_kernel, s0, step_pairs), grid_spe...]
    all_to_all x1 -> x4, waiting for transfers between devices: 722 us -> 631 us  [on_device(): moved = lax.all_to_all(sent, 'blk', split_axis=0, concat_axis=0, tiled=True)]
    transpose x1 -> x0, local copies, waits for them, and re-layouts: 42.3 us -> none  [on_device(): kv_cache.reshape(layers, 2, batch, local_rows, heads, HEAD_DIM)]
    unnamed x25 -> x19, local copies, waits for them, and re-layouts: 45.2 us -> 14 us
    psum x1 -> x0, waiting for transfers between devices: 30.1 us -> none  [on_device(): lax.psum((total * scale_factor, weighted * scale_factor[..., None]), 'seq')]
    convert_element_type x3 -> x0, other arithmetic: 24.5 us -> none  [the longest x1 23.3 us: on_device(): (grouped.astype(jnp.float32) / block_scale[..., None, None]).astype(jnp.b...]
    convert_element_type x2 -> x1, local copies, waits for them, and re-layouts: 23.6 us -> 0.03 us  [on_device(): fresh = fresh_key_value.transpose(0, 2, 1, 3).astype(jnp.float32)]
    all_to_all x1 -> x0, local copies, waits for them, and re-layouts: 23 us -> none  [on_device(): lax.all_to_all(arranged, 'blk', split_axis=2, concat_axis=3, tiled=True)]
  transfers between devices with their start and end apart: 2 -> 4, of which waited for: 2 -> 4; matrix products, arithmetic and copies ran while one was open for 0% -> 0% of each run, Pallas kernels for 0% -> 11%
where the time goes in v1:
time: 788 us; the launch traced here: 786 us
  waiting for transfers between devices  631 us (80%)
  Pallas kernels  116 us (15%)
  starting transfers between devices  22.7 us (3%)
  local copies, waits for them, and re-layouts  14.8 us (2%)
    all_to_all x4, waiting for transfers between devices, on_device(): moved = lax.all_to_all(sent, 'blk', split_axis=0, concat_axis=0, tiled=True)  631 us
    pallas_call x4, Pallas kernels, attend(): pl.pallas_call(functools.partial(attend_kernel, s0, step_pairs), grid_spe...  48.5 us
    pallas_call x2, Pallas kernels, combine(): pl.pallas_call(combine_kernel, in_specs=[pl.BlockSpec(memory_space=pltpu....  44.2 us
    pallas_call x4, Pallas kernels, gather_parts(): pl.pallas_call(gather_kernel, grid=(owners,), in_specs=[pl.BlockSpec((1,...  23.4 us
    all_to_all x4, starting transfers between devices, on_device(): moved = lax.all_to_all(sent, 'blk', split_axis=0, concat_axis=0, tiled=True)  22.7 us
  transfers between devices with their start and end apart: 4, of which 4 were waited for; matrix products, arithmetic and copies ran while one was open for 0% of the time, Pallas kernels for 11%

profile of v1, /device:TPU:1, one launch (start us, length us, event | category | flops | bytes accessed | tf_op | source)
XLA Modules:
  0.0 786.3 jit_solution(579773499374202253)
XLA Ops:
  0.6 5.9 shard_map.70
  6.5 3.4 copy-done.4
  9.9 6.3 all-to-all-start.3
  16.3 5.9 shard_map.69
  22.1 3.2 copy-done.2
  25.4 173.3 %all-to-all-done.3.x_ref = bf16[8,2,16,128,128]{4,3,2,1,0:T(8,128)(2,1)} async-done(((bf16[8,2,16,128,128]{4,3,2,1,0:T(8,128)(2,1)}), bf16[8,2,16,128,128]{4,3,2,1,0:T(8,128)(2,1)}, u32[]{:S(2)}, u32[]{:S(2)}) %all-to-all-start.3) | async-done | bytes 8388640 | tf_op jit(solution)/shard_map/all_to_all | solution.py:244
  198.6 5.0 all-to-all-start.2
  203.6 5.9 shard_map.68
  209.5 3.4 copy-done.3
  212.9 172.2 %all-to-all-done.2.x_ref = bf16[8,2,16,128,128]{4,3,2,1,0:T(8,128)(2,1)} async-done(((bf16[8,2,16,128,128]{4,3,2,1,0:T(8,128)(2,1)}), bf16[8,2,16,128,128]{4,3,2,1,0:T(8,128)(2,1)}, u32[]{:S(2)}, u32[]{:S(2)}) %all-to-all-start.2) | async-done | bytes 8388640 | tf_op jit(solution)/shard_map/all_to_all | solution.py:244
  385.1 5.4 all-to-all-start.1
  390.5 5.9 shard_map.67
  396.4 3.2 copy-done.1
  399.6 172.1 %all-to-all-done.1.x_ref = bf16[8,2,16,128,128]{4,3,2,1,0:T(8,128)(2,1)} async-done(((bf16[8,2,16,128,128]{4,3,2,1,0:T(8,128)(2,1)}), bf16[8,2,16,128,128]{4,3,2,1,0:T(8,128)(2,1)}, u32[]{:S(2)}, u32[]{:S(2)}) %all-to-all-start.1) | async-done | bytes 8388640 | tf_op jit(solution)/shard_map/all_to_all | solution.py:244
  571.7 5.9 all-to-all-start
  578.5 12.1 %shard_map.71 = (bf16[4,2,16,1024,128]{4,3,2,1,0:T(8,128)(2,1)}, f32[16,2,8]{2,1,0:T(2,128)S(1)}, f32[16,2,8,128]{3,2,1,0:T(8,128)S(1)}) custom-call(s32[16]{0:T(128)S(1)} %broadcast_subtract_fusion.left_ref, bf16[8,2,16,128,128]{4,3,2,1,0:T(8,128)(2,1)} %all-to-all-done.3.x_ref, bf16[4,16,8,128]{3,2,1,0:T(8,128)(2,1)S(1)} %bitcast.25), custom_call_target="tpu_custom_call" | custom-call | flops 268435456 | bytes 16777216 | tf_op jit(solution)/shard_map/pallas_call | solution.py:126
  590.6 12.1 %shard_map.72 = (bf16[4,2,16,1024,128]{4,3,2,1,0:T(8,128)(2,1)}, f32[16,2,8]{2,1,0:T(2,128)S(1)}, f32[16,2,8,128]{3,2,1,0:T(8,128)S(1)}) custom-call(s32[16]{0:T(128)S(1)} %broadcast_subtract_fusion.left_ref, bf16[8,2,16,128,128]{4,3,2,1,0:T(8,128)(2,1)} %all-to-all-done.2.x_ref, ...), custom_call_target="tpu_custom_call", output_to_operand_aliasing={{0}: (3, {})} | custom-call | flops 268435456 | bytes 16777216 | tf_op jit(solution)/shard_map/pallas_call | solution.py:126
  602.8 12.1 %shard_map.73 = (bf16[4,2,16,1024,128]{4,3,2,1,0:T(8,128)(2,1)}, f32[16,2,8]{2,1,0:T(2,128)S(1)}, f32[16,2,8,128]{3,2,1,0:T(8,128)S(1)}) custom-call(s32[16]{0:T(128)S(1)} %broadcast_subtract_fusion.left_ref, bf16[8,2,16,128,128]{4,3,2,1,0:T(8,128)(2,1)} %all-to-all-done.1.x_ref, ...), custom_call_target="tpu_custom_call", output_to_operand_aliasing={{0}: (3, {})} | custom-call | flops 268435456 | bytes 16777216 | tf_op jit(solution)/shard_map/pallas_call | solution.py:126
  614.9 30.6 %shard_map.75 = bf16[48,8,128]{2,1,0:T(8,128)(2,1)S(1)} custom-call(f32[48,2,8,128]{3,2,1,0:T(8,128)S(1)} %pad_maximum_fusion.stat_ref, bf16[48,8,128]{2,1,0:T(8,128)(2,1)S(1)} %bitcast.29, f32[48,2,128]{2,1,0:T(2,128)S(1)} %bitcast.30), custom_call_target="tpu_custom_call" | custom-call | bytes 1572864 | tf_op jit(solution)/shard_map/pallas_call | solution.py:207
  645.6 113.6 %all-to-all-done.x_ref = bf16[8,2,16,128,128]{4,3,2,1,0:T(8,128)(2,1)} async-done(((bf16[8,2,16,128,128]{4,3,2,1,0:T(8,128)(2,1)}), bf16[8,2,16,128,128]{4,3,2,1,0:T(8,128)(2,1)}, u32[]{:S(2)}, u32[]{:S(2)}) %all-to-all-start) | async-done | bytes 8388640 | tf_op jit(solution)/shard_map/all_to_all | solution.py:244
  759.1 12.1 %shard_map.74 = (bf16[4,2,16,1024,128]{4,3,2,1,0:T(8,128)(2,1)}, f32[16,2,8]{2,1,0:T(2,128)S(1)}, f32[16,2,8,128]{3,2,1,0:T(8,128)S(1)}) custom-call(s32[16]{0:T(128)S(1)} %broadcast_subtract_fusion.left_ref, bf16[8,2,16,128,128]{4,3,2,1,0:T(8,128)(2,1)} %all-to-all-done.x_ref, ...), custom_call_target="tpu_custom_call", output_to_operand_aliasing={{0}: (3, {})} | custom-call | flops 268435456 | bytes 16777216 | tf_op jit(solution)/shard_map/pallas_call | solution.py:126
  771.2 13.6 %shard_map.76 = bf16[16,8,128]{2,1,0:T(8,128)(2,1)S(1)} custom-call(f32[16,2,8,128]{3,2,1,0:T(8,128)S(1)} %get-tuple-element.26.stat_ref, bf16[16,8,128]{2,1,0:T(8,128)(2,1)S(1)} %bitcast.31, f32[16,2,128]{2,1,0:T(2,128)S(1)} %slice_bitcast_fusion.1.fresh_ref), custom_call_target="tpu_custom_call" | custom-call | bytes 524288 | tf_op jit(solution)/shard_map/pallas_call | solution.py:207
  784.9 0.7 copy.15
  785.6 0.7 pad_maximum_fusion.1
  (26 shorter events, 0.9 us)
Async XLA Ops:
  0.6 577.2 %copy-start = (s32[16]{0:T(128)S(1)}, s32[16]{0:T(128)}, u32[]{:S(2)}) copy-start(s32[16]{0:T(128)} %param.7) | copy-start | bytes 196
  6.5 3.4 copy-start.4
  9.9 188.7 %all-to-all-start.3 = ((bf16[8,2,16,128,128]{4,3,2,1,0:T(8,128)(2,1)}), bf16[8,2,16,128,128]{4,3,2,1,0:T(8,128)(2,1)}, u32[]{:S(2)}, u32[]{:S(2)}) async-start(bf16[8,2,16,128,128]{4,3,2,1,0:T(8,128)(2,1)} %copy-done.4), calls=%async_computation.3 | async-start | bytes 16777216 | tf_op jit(solution)/shard_map/all_to_all | solution.py:244
  22.1 3.2 copy-start.2
  198.6 186.5 %all-to-all-start.2 = ((bf16[8,2,16,128,128]{4,3,2,1,0:T(8,128)(2,1)}), bf16[8,2,16,128,128]{4,3,2,1,0:T(8,128)(2,1)}, u32[]{:S(2)}, u32[]{:S(2)}) async-start(bf16[8,2,16,128,128]{4,3,2,1,0:T(8,128)(2,1)} %copy-done.2), calls=%async_computation.2 | async-start | bytes 16777216 | tf_op jit(solution)/shard_map/all_to_all | solution.py:244
  209.5 3.4 copy-start.3
  385.1 186.6 %all-to-all-start.1 = ((bf16[8,2,16,128,128]{4,3,2,1,0:T(8,128)(2,1)}), bf16[8,2,16,128,128]{4,3,2,1,0:T(8,128)(2,1)}, u32[]{:S(2)}, u32[]{:S(2)}) async-start(bf16[8,2,16,128,128]{4,3,2,1,0:T(8,128)(2,1)} %copy-done.3), calls=%async_computation.1 | async-start | bytes 16777216 | tf_op jit(solution)/shard_map/all_to_all | solution.py:244
  396.3 3.2 copy-start.1
  399.6 178.1 %copy-start.5 = (bf16[4,16,1024]{2,1,0:T(8,128)(2,1)S(1)}, bf16[4,16,1024]{2,1,0:T(8,128)(2,1)}, u32[]{:S(2)}) copy-start(bf16[4,16,1024]{2,1,0:T(8,128)(2,1)} %param.5) | copy-start | bytes 393220
  399.6 178.1 %copy-start.6 = (bf16[4,2,16,128]{3,2,1,0:T(8,128)(2,1)S(1)}, bf16[4,2,16,128]{3,2,1,0:T(8,128)(2,1)}, u32[]{:S(2)}) copy-start(bf16[4,2,16,128]{3,2,1,0:T(8,128)(2,1)} %param.6) | copy-start | bytes 98308
  571.7 187.4 %all-to-all-start = ((bf16[8,2,16,128,128]{4,3,2,1,0:T(8,128)(2,1)}), bf16[8,2,16,128,128]{4,3,2,1,0:T(8,128)(2,1)}, u32[]{:S(2)}, u32[]{:S(2)}) async-start(bf16[8,2,16,128,128]{4,3,2,1,0:T(8,128)(2,1)} %copy-done.1), calls=%async_computation | async-start | bytes 16777216 | tf_op jit(solution)/shard_map/all_to_all | solution.py:244

commit v2 on v1

--- a/solution.py
+++ b/solution.py
@@ -13,34 +13,113 @@
 MESH = pl.DeviceIdType.MESH
 
 
-def gather_kernel(x_ref, o_ref):
-    o_ref[0] = x_ref[0]
-
-
-def gather_parts(kv_cache, layer, s0, ns, owners):
-    layers, _, batch, rows, width = kv_cache.shape
-    pairs = (width // HEAD_DIM) * batch // owners
-
-    def in_map(j):
-        first = j * pairs + s0
-        return (layer, 0, (first % batch) // ns, 0, first // batch)
-
-    shape = (owners, 2, ns, rows, HEAD_DIM)
-    size = owners * 2 * ns * rows * HEAD_DIM * 2
+def hand_over_kernel(
+    kv_ref, moved_ref, tail_ref, own, held, send_sem, recv_sem, own_in, own_out, tail_in, tail_out
+):
+    owners = lax.axis_size("blk")
+    me = lax.axis_index("blk")
+    _, units, _, ns, _, _ = moved_ref.shape
+    layers, _, batch, _, width = kv_ref.shape
+    halves = (units + 1) // layers
+    pairs = halves * ns
+
+    def part(owner, unit):
+        first = owner * pairs + (unit % halves) * ns
+        head = pl.multiple_of((first // batch) * HEAD_DIM, HEAD_DIM)
+        return kv_ref.at[
+            unit // halves, :, pl.ds(first % batch, ns), :, pl.ds(head, HEAD_DIM)
+        ]
+
+    bits = owners.bit_length() - 1
+
+    def partner(k):
+        if owners != 1 << bits:
+            return (me + k) % owners
+        peer = me + k
+        for b in range(bits):
+            peer = peer - 2 * (1 << b) * ((me // (1 << b)) % 2) * ((k // (1 << b)) % 2)
+        return peer
+
+    def send(unit, k):
+        peer = partner(k)
+        return pltpu.make_async_remote_copy(
+            src_ref=part(peer, unit),
+            dst_ref=moved_ref.at[me, unit],
+            send_sem=send_sem.at[unit, k - 1],
+            recv_sem=recv_sem.at[unit, k - 1],
+            device_id={"blk": peer},
+            device_id_type=MESH,
+        )
+
+    def loop(lo, hi, act):
+        def step(i, carry):
+            act(i)
+            return carry
+
+        lax.fori_loop(lo, hi, step, 0)
+
+    barrier = pltpu.get_barrier_semaphore()
+    loop(
+        1,
+        owners,
+        lambda k: pl.semaphore_signal(
+            barrier, inc=1, device_id={"blk": (me + k) % owners}, device_id_type=MESH
+        ),
+    )
+    pl.semaphore_wait(barrier, owners - 1)
+    loop(0, units, lambda u: loop(1, owners, lambda k: send(u, k).start()))
+
+    take_own = lambda u: pltpu.make_async_copy(part(me, u), own.at[u], own_in.at[u])
+    give_own = lambda u: pltpu.make_async_copy(own.at[u], moved_ref.at[me, u], own_out.at[u])
+    take_tail = lambda j: pltpu.make_async_copy(part(j, units), held.at[j], tail_in.at[j])
+    give_tail = lambda j: pltpu.make_async_copy(held.at[j], tail_ref.at[j], tail_out.at[j])
+    loop(0, owners, lambda j: take_tail(j).start())
+    loop(0, units, lambda u: take_own(u).start())
+    loop(0, owners, lambda j: take_tail(j).wait())
+    loop(0, owners, lambda j: give_tail(j).start())
+    loop(0, units, lambda u: take_own(u).wait())
+    loop(0, units, lambda u: give_own(u).start())
+    loop(0, owners, lambda j: give_tail(j).wait())
+    loop(0, units, lambda u: give_own(u).wait())
+    loop(0, units, lambda u: loop(1, owners, lambda k: send(u, k).wait()))
+
+
+def hand_over(kv_cache, units, ns):
+    rows = kv_cache.shape[3]
+    owners = lax.axis_size("blk")
+    piece = (2, ns, rows, HEAD_DIM)
+    dtype = kv_cache.dtype
+    dma = pltpu.SemaphoreType.DMA
     return pl.pallas_call(
-        gather_kernel,
-        grid=(owners,),
-        in_specs=[pl.BlockSpec((1, 2, ns, rows, HEAD_DIM), in_map)],
-        out_specs=pl.BlockSpec((1, 2, ns, rows, HEAD_DIM), lambda j: (j, 0, 0, 0, 0)),
-        out_shape=jax.ShapeDtypeStruct(shape, kv_cache.dtype),
-        cost_estimate=pl.CostEstimate(flops=0, bytes_accessed=2 * size, transcendentals=0),
-        compiler_params=pltpu.CompilerParams(vmem_limit_bytes=16 << 20),
+        hand_over_kernel,
+        in_specs=[pl.BlockSpec(memory_space=pl.ANY)],
+        out_specs=[pl.BlockSpec(memory_space=pl.ANY)] * 2,
+        out_shape=[
+            jax.ShapeDtypeStruct((owners, units, *piece), dtype),
+            jax.ShapeDtypeStruct((owners, *piece), dtype),
+        ],
+        scratch_shapes=[
+            pltpu.VMEM((units, *piece), dtype),
+            pltpu.VMEM((owners, *piece), dtype),
+            dma((units, owners - 1)),
+            dma((units, owners - 1)),
+            dma((units,)),
+            dma((units,)),
+            dma((owners,)),
+            dma((owners,)),
+        ],
+        cost_estimate=pl.CostEstimate(
+            flops=0, bytes_accessed=4 * kv_cache.size, transcendentals=0
+        ),
+        compiler_params=pltpu.CompilerParams(
+            collective_id=2, has_side_effects=True, vmem_limit_bytes=60 << 20
+        ),
     )(kv_cache)
 
 
-def attend_kernel(s0, step_pairs, left_ref, x_ref, q_ref, *rest):
+def attend_kernel(unit0, halves, ns, step_pairs, left_ref, x_ref, q_ref, *rest):
     quant_ref, scale_ref, stat_ref = rest[-3:]
-    parts, _, _, rows, _ = x_ref.shape
+    parts, _, _, _, rows, _ = x_ref.shape
     blocks = parts * rows // BLOCK
     inverse = 1.0 / (float(HEAD_DIM) ** 0.5)
     per_block = max(1, BLOCK // rows)
@@ -51,12 +130,13 @@
         if rows >= BLOCK:
             inside = rows // BLOCK
             lo = (n % inside) * BLOCK
-            return x_ref[n // inside, c, s, lo : lo + BLOCK, :]
-        piece = x_ref[n * per_block : (n + 1) * per_block, c, s, :, :]
+            return x_ref[n // inside, 0, c, s, lo : lo + BLOCK, :]
+        piece = x_ref[n * per_block : (n + 1) * per_block, 0, c, s, :, :]
         return piece.reshape(BLOCK, HEAD_DIM)
 
+    start = ((unit0 + pl.program_id(0)) % halves) * ns + pl.program_id(1) * step_pairs
     for s in range(step_pairs):
-        live = left_ref[s0 + pl.program_id(0) * step_pairs + s]
+        live = left_ref[start + s]
         scales = [[], []]
         for c in range(2):
             row = jnp.zeros((1, blocks), jnp.float32)
@@ -104,17 +184,28 @@
         stat_ref[s, 1] = jnp.where(lane < BLOCK // 2, top, total)
 
 
-def attend(left, moved, queries, quant, out_shape, layer, s0):
-    owners, _, ns, rows, _ = moved.shape
+def attend(left, moved, queries, quant, out_shape, unit0):
+    owners, units, _, ns, rows, _ = moved.shape
     seq_rows = owners * rows
     blocks = seq_rows // BLOCK
+    halves = out_shape[2] // ns
     step_pairs = 2 if ns % 2 == 0 else 1
-    size = 2 * ns * seq_rows * HEAD_DIM * 2
-    first = s0 // step_pairs
+    steps = ns // step_pairs
+    size = units * 2 * ns * seq_rows * HEAD_DIM * 2
+
+    def layer(u):
+        return (unit0 + u) // halves
+
+    def place(u, i):
+        return ((unit0 + u) % halves) * steps + i
+
     in_specs = [
-        pl.BlockSpec((owners, 2, step_pairs, rows, HEAD_DIM), lambda i, left: (0, 0, i, 0, 0)),
         pl.BlockSpec(
-            (1, step_pairs, QUERY_GROUP, HEAD_DIM), lambda i, left: (layer, first + i, 0, 0)
+            (owners, 1, 2, step_pairs, rows, HEAD_DIM), lambda u, i, left: (0, u, 0, i, 0, 0)
+        ),
+        pl.BlockSpec(
+            (1, step_pairs, QUERY_GROUP, HEAD_DIM),
+            lambda u, i, left: (layer(u), place(u, i), 0, 0),
         ),
     ]
     operands = [left, moved, queries]
@@ -124,32 +215,33 @@
         operands.append(quant)
         aliases = {3: 0}
     return pl.pallas_call(
-        functools.partial(attend_kernel, s0, step_pairs),
+        functools.partial(attend_kernel, unit0, halves, ns, step_pairs),
         grid_spec=pltpu.PrefetchScalarGridSpec(
             num_scalar_prefetch=1,
-            grid=(ns // step_pairs,),
+            grid=(units, steps),
             in_specs=in_specs,
             out_specs=[
                 pl.BlockSpec(
                     (1, 2, step_pairs, seq_rows, HEAD_DIM),
-                    lambda i, left: (layer, 0, first + i, 0, 0),
+                    lambda u, i, left: (layer(u), 0, place(u, i), 0, 0),
                 ),
-                pl.BlockSpec((step_pairs, 2, blocks), lambda i, left: (i, 0, 0)),
+                pl.BlockSpec((step_pairs, 2, blocks), lambda u, i, left: (u * steps + i, 0, 0)),
                 pl.BlockSpec(
-                    (step_pairs, 2, QUERY_GROUP, HEAD_DIM), lambda i, left: (i, 0, 0, 0)
+                    (step_pairs, 2, QUERY_GROUP, HEAD_DIM),
+                    lambda u, i, left: (u * steps + i, 0, 0, 0),
                 ),
             ],
         ),
         out_shape=[
             jax.ShapeDtypeStruct(out_shape, jnp.bfloat16),
-            jax.ShapeDtypeStruct((ns, 2, blocks), jnp.float32),
-            jax.ShapeDtypeStruct((ns, 2, QUERY_GROUP, HEAD_DIM), jnp.float32),
+            jax.ShapeDtypeStruct((units * ns, 2, blocks), jnp.float32),
+            jax.ShapeDtypeStruct((units * ns, 2, QUERY_GROUP, HEAD_DIM), jnp.float32),
         ],
         input_output_aliases=aliases,
         cost_estimate=pl.CostEstimate(
             flops=4 * size * QUERY_GROUP, bytes_accessed=2 * size, transcendentals=0
         ),
-        compiler_params=pltpu.CompilerParams(vmem_limit_bytes=24 << 20),
+        compiler_params=pltpu.CompilerParams(vmem_limit_bytes=48 << 20),
     )(*operands)
 
 
@@ -234,32 +326,28 @@
     left = lengths[(first_pair + jnp.arange(pairs, dtype=jnp.int32)) % batch]
     left = left - lax.axis_index("seq") * seq_rows
     grouped = queries.reshape(layers, pairs, QUERY_GROUP, HEAD_DIM)
-    chunks = [(layer, 0, pairs) for layer in range(layers)]
     out_shape = (layers, 2, pairs, seq_rows, HEAD_DIM)
-
-    quant = None
-    scales, stats = [], []
-    for layer, s0, ns in chunks:
-        sent = gather_parts(kv_cache, layer, s0, ns, owners)
-        moved = lax.all_to_all(sent, "blk", split_axis=0, concat_axis=0, tiled=True)
-        quant, scale, stat = attend(left, moved, grouped, quant, out_shape, layer, s0)
-        scales.append(scale)
-        stats.append(stat)
+    halves = 2 if pairs % 2 == 0 else 1
+    ns = pairs // halves
+    units = layers * halves - 1
+
+    moved, tail = hand_over(kv_cache, units, ns)
+    tail = lax.all_to_all(tail, "blk", split_axis=0, concat_axis=0, tiled=True)
+    quant, scale, stat = attend(left, moved, grouped, None, out_shape, 0)
+    quant, last_scale, last_stat = attend(left, tail[:, None], grouped, quant, out_shape, units)
+    grouped = grouped.reshape(layers * pairs, QUERY_GROUP, HEAD_DIM)
     fresh = fresh_key_value.transpose(0, 2, 1, 3).astype(jnp.float32)
-    early = layers - 1
-    outs = []
-    for ident, (lo, hi) in enumerate([(0, early), (early, layers)]):
-        amount = (hi - lo) * pairs
-        outs.append(
-            combine(
-                jnp.concatenate(stats[lo:hi], axis=0),
-                grouped[lo:hi].reshape(amount, QUERY_GROUP, HEAD_DIM),
-                fresh[lo:hi].reshape(amount, 2, HEAD_DIM),
-                ident,
-            ).reshape(hi - lo, pairs, QUERY_GROUP * HEAD_DIM)
-        )
-    attended = jnp.concatenate(outs, axis=0)
-    block_scale = jnp.stack(scales).transpose(0, 2, 1, 3)
+    fresh = fresh.reshape(layers * pairs, 2, HEAD_DIM)
+    cut = units * ns
+    attended = jnp.concatenate(
+        [
+            combine(stat, grouped[:cut], fresh[:cut], 0),
+            combine(last_stat, grouped[cut:], fresh[cut:], 1),
+        ],
+        axis=0,
+    ).reshape(layers, pairs, QUERY_GROUP * HEAD_DIM)
+    block_scale = jnp.concatenate([scale, last_scale], axis=0)
+    block_scale = block_scale.reshape(layers, pairs, 2, blocks).transpose(0, 2, 1, 3)
     return quant, block_scale, attended
 
 

time: 788 us -> 777 us (0.986)
  waiting for transfers between devices: 631 us -> 18.5 us
  Pallas kernels: 116 us -> 725 us
  local copies, waits for them, and re-layouts: 14.8 us -> 2.32 us
    all_to_all x4 -> x1, waiting for transfers between devices: 631 us -> 18.5 us  [on_device(): tail = lax.all_to_all(tail, 'blk', split_axis=0, concat_axis=0, tiled=True)]
    pallas_call x8 -> x3, Pallas kernels: 71.9 us -> 681 us  [the longest x1 637 us: hand_over(): pl.pallas_call(hand_over_kernel, in_specs=[pl.BlockSpec(memory_space=pl.A...]
    unnamed x19 -> x7, local copies, waits for them, and re-layouts: 14 us -> 0.04 us
    all_to_all x4 -> x1, starting transfers between devices: 22.7 us -> 28.8 us  [on_device(): tail = lax.all_to_all(tail, 'blk', split_axis=0, concat_axis=0, tiled=True)]
  transfers between devices with their start and end apart: 4 -> 1, of which waited for: 4 -> 1; matrix products, arithmetic and copies ran while one was open for 0% -> 0% of each run, Pallas kernels for 11% -> 9%
where the time goes in v2:
time: 777 us; the launch traced here: 776 us
  Pallas kernels  725 us (93%)
  starting transfers between devices  28.8 us (4%)
  waiting for transfers between devices  18.5 us (2%)
    pallas_call x1, Pallas kernels, hand_over(): pl.pallas_call(hand_over_kernel, in_specs=[pl.BlockSpec(memory_space=pl.A...  637 us
    pallas_call x2, Pallas kernels, attend(): pl.pallas_call(functools.partial(attend_kernel, unit0, halves, ns, step_p...  44.6 us
    pallas_call x2, Pallas kernels, combine(): pl.pallas_call(combine_kernel, in_specs=[pl.BlockSpec(memory_space=pltpu....  43.9 us
    all_to_all x1, starting transfers between devices, on_device(): tail = lax.all_to_all(tail, 'blk', split_axis=0, concat_axis=0, tiled=True)  28.8 us
    all_to_all x1, waiting for transfers between devices, on_device(): tail = lax.all_to_all(tail, 'blk', split_axis=0, concat_axis=0, tiled=True)  18.5 us
  transfers between devices with their start and end apart: 1, of which 1 were waited for; matrix products, arithmetic and copies ran while one was open for 0% of the time, Pallas kernels for 9%

profile of v2, /device:TPU:1, one launch (start us, length us, event | category | flops | bytes accessed | tf_op | source)
XLA Modules:
  0.0 775.6 jit_solution(6037878201195023764)
XLA Ops:
  0.6 0.0 copy-start
  0.6 0.0 copy-start.2
  0.7 0.0 copy-start.1
  0.7 636.6 %shard_map.67 = (bf16[8,7,2,8,128,128]{5,4,3,2,1,0:T(8,128)(2,1)}, bf16[8,2,8,128,128]{4,3,2,1,0:T(8,128)(2,1)}) custom-call(bf16[4,2,16,128,1024]{4,3,2,1,0:T(8,128)(2,1)} %kv_ref.1), custom_call_target="tpu_custom_call" | custom-call | bytes 67108864 | tf_op jit(solution)/shard_map/pallas_call | solution.py:93
  637.3 28.8 %all-to-all-start = ((bf16[8,2,8,128,128]{4,3,2,1,0:T(8,128)(2,1)}), bf16[8,2,8,128,128]{4,3,2,1,0:T(8,128)(2,1)}, u32[]{:S(2)}, u32[]{:S(2)}) async-start(bf16[8,2,8,128,128]{4,3,2,1,0:T(8,128)(2,1)} %get-tuple-element.11), calls=%async_computation | async-start | bytes 8388608 | tf_op jit(solution)/shard_map/all_to_all | solution.py:335
  666.1 0.0 copy-done.2
  666.2 0.0 copy-done.1
  666.3 0.0 copy-done
  666.3 0.7 gather_fusion
  666.9 37.5 %shard_map.68 = (bf16[4,2,16,1024,128]{4,3,2,1,0:T(8,128)(2,1)}, f32[56,2,8]{2,1,0:T(2,128)S(1)}, f32[56,2,8,128]{3,2,1,0:T(8,128)S(1)}) custom-call(s32[16]{0:T(128)S(1)} %broadcast_subtract_fusion.left_ref, bf16[8,7,2,8,128,128]{5,4,3,2,1,0:T(8,128)(2,1)} %get-tuple-element.12.x_ref, bf16[4,16,8,128]{3,2,1,0:T(8,128)(2,1)S(1)} %bitcast.20), custom_call_target="tpu_custom_call" | custom-call | flops 939524096 | bytes 58720256 | tf_op jit(solution)/shard_map/pallas_call | solution.py:217
  704.5 0.1 copy.12
  704.5 34.7 %shard_map.70 = bf16[56,8,128]{2,1,0:T(8,128)(2,1)S(1)} custom-call(f32[56,2,8,128]{3,2,1,0:T(8,128)S(1)} %get-tuple-element.17.stat_ref, bf16[56,8,128]{2,1,0:T(8,128)(2,1)S(1)} %slice.18.q_ref, f32[56,2,128]{2,1,0:T(2,128)S(1)} %slice.19.fresh_ref), custom_call_target="tpu_custom_call" | custom-call | bytes 1835008 | tf_op jit(solution)/shard_map/pallas_call | solution.py:299
  739.3 18.5 %all-to-all-done = bf16[8,2,8,128,128]{4,3,2,1,0:T(8,128)(2,1)} async-done(((bf16[8,2,8,128,128]{4,3,2,1,0:T(8,128)(2,1)}), bf16[8,2,8,128,128]{4,3,2,1,0:T(8,128)(2,1)}, u32[]{:S(2)}, u32[]{:S(2)}) %all-to-all-start) | async-done | bytes 4194336 | tf_op jit(solution)/shard_map/all_to_all | solution.py:335
  757.8 7.0 shard_map.69
  764.8 9.2 %shard_map.71 = bf16[8,8,128]{2,1,0:T(8,128)(2,1)S(1)} custom-call(f32[8,2,8,128]{3,2,1,0:T(8,128)S(1)} %get-tuple-element.18.stat_ref, bf16[8,8,128]{2,1,0:T(8,128)(2,1)S(1)} %slice.20.q_ref, f32[8,2,128]{2,1,0:T(2,128)S(1)} %slice.21.fresh_ref), custom_call_target="tpu_custom_call" | custom-call | bytes 262144 | tf_op jit(solution)/shard_map/pallas_call | solution.py:299
  774.0 0.7 reshape.74
  774.8 0.1 copy.13
  774.8 0.1 pad_maximum_fusion.1
  774.9 0.1 reshape.71
  775.0 0.6 copy.19
  (11 shorter events, 0.1 us)
Async XLA Ops:
  0.6 665.6 %copy-start = (s32[16]{0:T(128)S(1)}, s32[16]{0:T(128)}, u32[]{:S(2)}) copy-start(s32[16]{0:T(128)} %param.7) | copy-start | bytes 196
  0.6 665.4 %copy-start.2 = (bf16[4,2,16,128]{3,2,1,0:T(8,128)(2,1)S(1)}, bf16[4,2,16,128]{3,2,1,0:T(8,128)(2,1)}, u32[]{:S(2)}) copy-start(bf16[4,2,16,128]{3,2,1,0:T(8,128)(2,1)} %param.6) | copy-start | bytes 98308
  0.7 665.5 %copy-start.1 = (bf16[4,16,1024]{2,1,0:T(8,128)(2,1)S(1)}, bf16[4,16,1024]{2,1,0:T(8,128)(2,1)}, u32[]{:S(2)}) copy-start(bf16[4,16,1024]{2,1,0:T(8,128)(2,1)} %param.5) | copy-start | bytes 393220
  637.3 120.5 %all-to-all-start = ((bf16[8,2,8,128,128]{4,3,2,1,0:T(8,128)(2,1)}), bf16[8,2,8,128,128]{4,3,2,1,0:T(8,128)(2,1)}, u32[]{:S(2)}, u32[]{:S(2)}) async-start(bf16[8,2,8,128,128]{4,3,2,1,0:T(8,128)(2,1)} %get-tuple-element.11), calls=%async_computation | async-start | bytes 8388608 | tf_op jit(solution)/shard_map/all_to_all | solution.py:335
